TPU v7x, 32 devices: a whole 2x2x4 slice. The times are simulated.
32 devices in a mesh: row: 8 (over y, x, core), col: 4 (over z).
Axes of the slice: x: 2, y: 2, z: 4, core: 2. Of those that a mesh axis runs over, the one named last changes fastest.
Arguments:
- choi: float32 [4, 2048, 1024], P(None, 'row', 'col'), may hold values from -0.5 to 8, as said below
Outputs:
- factored: float32 [4, 2048, 1024], P(None, 'row', 'col')
Inputs may be any that keep to these rules, and one draw needn't show every extreme that they name: `choi`: the leading 1024 x 1024 block of the matrix is symmetric with a positive diagonal, and its leading 2 * 256 square is positive definite.
All inputs are finite; a program needn't handle non-finite values.
Results may differ from a plain program's by a relative error of at most 0.0001.
Values sent between devices are 32-bit elements; how exact they have to be, the bound alone decides.
A program may use at most 64 MiB of HBM per device.

v0:
```python
import jax
import jax.numpy as jnp
from jax import lax
from jax.sharding import PartitionSpec as P

PANELS = 2


def broadcast(value, axis, source):
    kept = jnp.where(lax.axis_index(axis) == source, value, 0).astype(value.dtype)
    return lax.psum(kept, axis)


def factor_tile(diagonal):
    tile_size = diagonal.shape[0]
    identity = jnp.eye(tile_size, dtype=jnp.float32)
    factor = jnp.linalg.cholesky(diagonal)
    inverse = jax.scipy.linalg.solve_triangular(factor, identity, lower=True)
    return (factor, inverse)


def panel_from(blocks, factor, inverse, tile_index, step):
    beneath = jnp.einsum("sij,kj->sik", blocks, inverse, precision=lax.Precision.HIGHEST)
    place = tile_index[:, None, None]
    return jnp.where(place > step, beneath, jnp.where(place == step, factor[None], 0.0))


def body(choi):
    slot_count = choi.shape[0]
    row_count = lax.axis_size("row")
    my_row = lax.axis_index("row")
    my_col = lax.axis_index("col")
    tile_index = jnp.arange(slot_count, dtype=jnp.int32) * row_count + my_row
    current = choi
    for step in range(PANELS):
        row_tile = current[step // row_count]
        tile_row = broadcast(row_tile, "row", step % row_count)

        def build(operands):
            factor, inverse = factor_tile(operands[0])
            return panel_from(operands[1], factor, inverse, tile_index, step)

        def nothing(operands):
            return jnp.zeros_like(operands[1])

        panel_tiles = lax.cond(my_col == step, build, nothing, (tile_row, current))
        panel_tiles = broadcast(panel_tiles, "col", step)
        my_tile = lax.dynamic_index_in_dim(panel_tiles, my_col // row_count, 0, keepdims=False)
        partner = broadcast(my_tile, "row", my_col % row_count)
        updated = current - jnp.einsum(
            "sij,kj->sik", panel_tiles, partner, precision=lax.Precision.HIGHEST
        )
        trailing = (tile_index[:, None, None] > step) & (my_col > step)
        current = jnp.where(my_col == step, panel_tiles, jnp.where(trailing, updated, current))
    cleared = (my_col >= PANELS) & (tile_index[:, None, None] < PANELS)
    return jnp.where(cleared, 0.0, current)


def solution(mesh):
    return jax.shard_map(
        body,
        mesh=mesh,
        in_specs=(P(None, "row", "col"),),
        out_specs=P(None, "row", "col"),
        check_vma=False,
    )
```

profile of v0, /device:TPU:0, one launch (start us, length us, event | category | flops | bytes accessed | tf_op | source)
XLA Modules:
  0.0 474.8 jit_solution(8787741748421579258)
XLA Ops:
  6.5 1.7 select_bitcast_fusion.4
  8.3 58.7 %all-reduce.8.cloned.1.call-done = f32[256,256]{1,0:T(8,128)} async-done(((f32[256,256]{1,0:T(8,128)}), f32[256,256]{1,0:T(8,128)}) %all-reduce.8.cloned.1.call-update) | async-done | bytes 262160 | tf_op jit(solution)/shard_map/psum | solution.py:11
  67.0 63.7 %conditional.2 = (f32[4,256,256]{2,1,0:T(8,128)S(1)}) conditional(s32[]{:T(128)} %convert_element_type.21, () %tuple.20, (s32[4]{0:T(128)S(1)}, f32[256,256]{1,0:T(8,128)}, f32[4,256,256]{2,1,0:T(8,128)}) %tuple.21), branch_computations={%region_1.2_spmd, %region_2.9_spmd} | conditional | flops 1007927552 | bytes 15337775 | solution.py:46
  67.1 0.8 copy-done.2
  68.2 11.7 %cholesky.130 = f32[128,128]{1,0:T(8,128)S(1)} custom-call(f32[128,128]{1,0:T(8,128)S(1)} %cholesky.194), custom_call_target="Cholesky" | custom-call | tf_op jit(solution)/shard_map/cond/branch_1_fun/jit(cholesky)/cholesky | solution.py:17
  79.9 9.8 %custom-call.13 = f32[1,128,128]{1,2,0:T(8,128)S(1)} custom-call(f32[1,128,128]{2,1,0:T(8,128)S(1)} %get-tuple-element.82), custom_call_target="InvertDiagBlocksLowerTriangular" | custom-call | tf_op jit(solution)/shard_map/cond/branch_1_fun/jit(cholesky)/cholesky | solution.py:17
  90.2 11.7 %cholesky.147 = f32[128,128]{1,0:T(8,128)S(1)} custom-call(f32[128,128]{1,0:T(8,128)S(1)} %convolution_subtract_fusion.1), custom_call_target="Cholesky" | custom-call | tf_op jit(solution)/shard_map/cond/branch_1_fun/jit(cholesky)/cholesky | solution.py:17
  104.2 4.3 while.4
  105.0 1.4 bitcast_dynamic-update-slice_fusion.5
  107.1 1.4 bitcast_dynamic-update-slice_fusion.5
  108.5 19.7 %custom-call.14 = f32[2,128,128]{1,2,0:T(8,128)S(1)} custom-call(f32[2,128,128]{2,1,0:T(8,128)S(1)} %get-tuple-element.45), custom_call_target="InvertDiagBlocksLowerTriangular" | custom-call | tf_op jit(solution)/shard_map/cond/branch_1_fun/jit(_solve_triangular)/triangular_solve | solution.py:18
  129.1 1.1 fusion
  130.8 1.1 broadcast_select_fusion.1
  131.9 48.6 %all-reduce.10.cloned.1.call-done = f32[4,256,256]{2,1,0:T(8,128)} async-done(((f32[4,256,256]{2,1,0:T(8,128)}), f32[4,256,256]{2,1,0:T(8,128)}) %all-reduce.10.cloned.1.call-update) | async-done | bytes 1048592 | tf_op jit(solution)/shard_map/psum | solution.py:11
  180.5 1.7 select_bitcast_fusion.3
  182.3 54.5 %all-reduce.12.cloned.1.call-done = f32[256,256]{1,0:T(8,128)} async-done(((f32[256,256]{1,0:T(8,128)}), f32[256,256]{1,0:T(8,128)}) %all-reduce.12.cloned.1.call-update) | async-done | bytes 262160 | tf_op jit(solution)/shard_map/psum | solution.py:11
  236.8 2.7 fusion.32
  239.5 0.7 fusion.33
  240.3 53.4 %all-reduce.14.cloned.1.call-done = f32[256,256]{1,0:T(8,128)} async-done(((f32[256,256]{1,0:T(8,128)}), f32[256,256]{1,0:T(8,128)}) %all-reduce.14.cloned.1.call-update) | async-done | bytes 262160 | tf_op jit(solution)/shard_map/psum | solution.py:11
  294.1 1.1 broadcast_select_fusion
  295.2 113.0 %all-reduce.16.cloned.1.call-done = f32[4,256,256]{2,1,0:T(8,128)} async-done(((f32[4,256,256]{2,1,0:T(8,128)}), f32[4,256,256]{2,1,0:T(8,128)}) %all-reduce.16.cloned.1.call-update) | async-done | bytes 1048592 | tf_op jit(solution)/shard_map/psum | solution.py:11
  408.2 1.7 select_bitcast_fusion.2
  410.0 54.4 %all-reduce.18.cloned.1.call-done = f32[256,256]{1,0:T(8,128)} async-done(((f32[256,256]{1,0:T(8,128)}), f32[256,256]{1,0:T(8,128)}) %all-reduce.18.cloned.1.call-update) | async-done | bytes 262160 | tf_op jit(solution)/shard_map/psum | solution.py:11
  464.3 3.6 fusion.31
  (46 shorter events, 4.9 us)
Async XLA Ops:
  6.5 60.5 %all-reduce.8.cloned.1.call-start = ((), (), s32[]{:S(2)}) async-start(), calls=%async_computation | async-start | bytes 524288 | tf_op jit(solution)/shard_map/psum | solution.py:11
  8.2 172.3 %all-reduce.10.cloned.1.call-start = ((), (), s32[]{:S(2)}) async-start(), calls=%async_computation.1 | async-start | bytes 2097152 | tf_op jit(solution)/shard_map/psum | solution.py:11
  67.0 0.9 copy-start.2
  104.2 24.9 %copy-start.1 = (f32[4,256,256]{2,1,0:T(8,128)S(1)}, f32[4,256,256]{2,1,0:T(8,128)}, u32[]{:S(2)}) copy-start(f32[4,256,256]{2,1,0:T(8,128)} %get-tuple-element.26) | copy-start | bytes 3145732 | tf_op jit(solution)/shard_map/cond
  131.8 105.0 %copy-start = (f32[4,256,256]{2,1,0:T(8,128)S(1)}, f32[4,256,256]{2,1,0:T(8,128)}, u32[]{:S(2)}) copy-start(f32[4,256,256]{2,1,0:T(8,128)} %param.8) | copy-start | bytes 3145732
  131.9 104.9 %all-reduce.12.cloned.1.call-start = ((), (), s32[]{:S(2)}) async-start(), calls=%async_computation.2 | async-start | bytes 524288 | tf_op jit(solution)/shard_map/psum | solution.py:11
  182.2 111.4 %all-reduce.14.cloned.1.call-start = ((), (), s32[]{:S(2)}) async-start(), calls=%async_computation.3 | async-start | bytes 524288 | tf_op jit(solution)/shard_map/psum | solution.py:11
  240.2 168.0 %all-reduce.16.cloned.1.call-start = ((), (), s32[]{:S(2)}) async-start(), calls=%async_computation.4 | async-start | bytes 2097152 | tf_op jit(solution)/shard_map/psum | solution.py:11
  295.2 169.2 %all-reduce.18.cloned.1.call-start = ((), (), s32[]{:S(2)}) async-start(), calls=%async_computation.5 | async-start | bytes 524288 | tf_op jit(solution)/shard_map/psum | solution.py:11
Sparse Core Ops, SparseCore 0:
  10.4 56.5 all-reduce.7
  132.0 48.5 all-reduce.9
  183.6 53.1 all-reduce.11
  240.3 53.3 all-reduce.13
  295.9 112.3 all-reduce.15
  411.1 53.1 all-reduce.17
where the time goes:
time: 475 us
  waiting for transfers between devices  383 us (81%)
  other arithmetic  61.7 us (13%)
  between operations  13.6 us (3%)
  matrix products  8.71 us (2%)
  local copies, waits for them, and re-layouts  5.67 us (1%)
    psum x6, waiting for transfers between devices, broadcast(): return lax.psum(kept, axis)  383 us
    another operation x6, other arithmetic, factor_tile(): factor = jnp.linalg.cholesky(diagonal)  34 us
    another operation x4, other arithmetic, factor_tile(): inverse = jax.scipy.linalg.solve_triangular(factor, identity, lower=True)  19.7 us
  transfers between devices with their start and end apart: 6, of which 6 were waited for; matrix products, arithmetic and copies ran while one was open for 0% of the time, Pallas kernels for 0%

commit v1 on v0

--- a/solution.py
+++ b/solution.py
@@ -8,7 +8,11 @@
 
 def broadcast(value, axis, source):
     kept = jnp.where(lax.axis_index(axis) == source, value, 0).astype(value.dtype)
-    return lax.psum(kept, axis)
+
+    def cover_gates_here(frame):
+        return jnp.sum(lax.all_gather(frame, axis), axis=0)
+
+    return cover_gates_here(kept)
 
 
 def factor_tile(diagonal):

time: 475 us -> 430 us (0.905)
  waiting for transfers between devices: 383 us -> 333 us
  other arithmetic: 61.7 us -> 70.2 us
    psum x6 -> x0, waiting for transfers between devices: 383 us -> none  [broadcast(): return lax.psum(kept, axis)]
    all_gather x0 -> x6, waiting for transfers between devices: none -> 333 us  [cover_gates_here(): return jnp.sum(lax.all_gather(frame, axis), axis=0)]
    reduce_sum x0 -> x5, other arithmetic: none -> 10.5 us  [cover_gates_here(): return jnp.sum(lax.all_gather(frame, axis), axis=0)]
where the time goes in v1:
time: 430 us
  waiting for transfers between devices  333 us (77%)
  other arithmetic  70.2 us (16%)
  between operations  13.6 us (3%)
  matrix products  5.43 us (1%)
  local copies, waits for them, and re-layouts  4.67 us (1%)
    all_gather x6, waiting for transfers between devices, cover_gates_here(): return jnp.sum(lax.all_gather(frame, axis), axis=0)  333 us
    another operation x6, other arithmetic, factor_tile(): factor = jnp.linalg.cholesky(diagonal)  34 us
    another operation x4, other arithmetic, factor_tile(): inverse = jax.scipy.linalg.solve_triangular(factor, identity, lower=True)  19.7 us
    reduce_sum x5, other arithmetic, cover_gates_here(): return jnp.sum(lax.all_gather(frame, axis), axis=0)  10.5 us
  transfers between devices with their start and end apart: 6, of which 6 were waited for; matrix products, arithmetic and copies ran while one was open for 0% of the time, Pallas kernels for 0%

profile of v1, /device:TPU:0, one launch (start us, length us, event | category | flops | bytes accessed | tf_op | source)
XLA Modules:
  0.0 429.6 jit_solution(13317623542121607462)
XLA Ops:
  6.5 1.7 slice_select_fusion.1
  8.3 31.5 %all-gather.9.cloned.1.call-done = f32[8,256,256]{2,1,0:T(8,128)} async-done(((f32[1,256,256]{2,1,0:T(8,128)}), f32[8,256,256]{2,1,0:T(8,128)}) %all-gather.9.cloned.1.call-update) | async-done | bytes 2097168 | tf_op jit(solution)/shard_map/all_gather | solution.py:13
  39.8 64.3 %conditional.2 = (f32[4,256,256]{2,1,0:T(8,128)S(1)}) conditional(s32[]{:T(128)} %convert_element_type.21, () %tuple.20, (s32[4]{0:T(128)S(1)}, f32[8,256,256]{2,1,0:T(8,128)}, f32[4,256,256]{2,1,0:T(8,128)}) %tuple.21), branch_computations={%region_0.1_spmd, %region_1.9_spmd} | conditional | flops 1008386304 | bytes 16648471 | solution.py:50
  39.8 1.8 reduce_sum.50
  41.8 11.7 %cholesky.130 = f32[128,128]{1,0:T(8,128)S(1)} custom-call(f32[128,128]{1,0:T(8,128)S(1)} %cholesky.194), custom_call_target="Cholesky" | custom-call | tf_op jit(solution)/shard_map/cond/branch_1_fun/jit(cholesky)/cholesky | solution.py:21
  53.6 9.8 %custom-call.13 = f32[1,128,128]{1,2,0:T(8,128)S(1)} custom-call(f32[1,128,128]{2,1,0:T(8,128)S(1)} %get-tuple-element.80), custom_call_target="InvertDiagBlocksLowerTriangular" | custom-call | tf_op jit(solution)/shard_map/cond/branch_1_fun/jit(cholesky)/cholesky | solution.py:21
  63.9 11.7 %cholesky.147 = f32[128,128]{1,0:T(8,128)S(1)} custom-call(f32[128,128]{1,0:T(8,128)S(1)} %convolution_subtract_fusion.1), custom_call_target="Cholesky" | custom-call | tf_op jit(solution)/shard_map/cond/branch_1_fun/jit(cholesky)/cholesky | solution.py:21
  77.8 4.1 while.4
  78.5 1.4 bitcast_dynamic-update-slice_fusion.5
  80.5 1.4 bitcast_dynamic-update-slice_fusion.5
  81.9 19.7 %custom-call.14 = f32[2,128,128]{1,2,0:T(8,128)S(1)} custom-call(f32[2,128,128]{2,1,0:T(8,128)S(1)} %get-tuple-element.49), custom_call_target="InvertDiagBlocksLowerTriangular" | custom-call | tf_op jit(solution)/shard_map/cond/branch_1_fun/jit(_solve_triangular)/triangular_solve | solution.py:22
  102.5 1.1 fusion
  104.1 1.1 broadcast_select_fusion.1
  105.3 78.1 %all-gather.17.cloned.1.call-done = f32[16,256,256]{2,1,0:T(8,128)} async-done(((f32[4,256,256]{2,1,0:T(8,128)}), f32[16,256,256]{2,1,0:T(8,128)}) %all-gather.17.cloned.1.call-update) | async-done | bytes 4194320 | tf_op jit(solution)/shard_map/all_gather | solution.py:13
  183.3 2.6 reduce_sum.56
  186.8 26.3 %all-gather.11.cloned.1.call-done = f32[8,256,256]{2,1,0:T(8,128)} async-done(((f32[1,256,256]{2,1,0:T(8,128)}), f32[8,256,256]{2,1,0:T(8,128)}) %all-gather.11.cloned.1.call-update) | async-done | bytes 2097168 | tf_op jit(solution)/shard_map/all_gather | solution.py:13
  213.1 1.8 reduce_sum.57
  216.7 27.9 %all-gather.13.cloned.1.call-done = f32[8,256,256]{2,1,0:T(8,128)} async-done(((f32[1,256,256]{2,1,0:T(8,128)}), f32[8,256,256]{2,1,0:T(8,128)}) %all-gather.13.cloned.1.call-update) | async-done | bytes 2097168 | tf_op jit(solution)/shard_map/all_gather | solution.py:13
  245.0 1.1 broadcast_select_fusion
  246.1 143.1 %all-gather.19.cloned.1.call-done = f32[16,256,256]{2,1,0:T(8,128)} async-done(((f32[4,256,256]{2,1,0:T(8,128)}), f32[16,256,256]{2,1,0:T(8,128)}) %all-gather.19.cloned.1.call-update) | async-done | bytes 4194320 | tf_op jit(solution)/shard_map/all_gather | solution.py:13
  389.2 2.6 reduce_sum.58
  392.6 26.4 %all-gather.15.cloned.1.call-done = f32[8,256,256]{2,1,0:T(8,128)} async-done(((f32[1,256,256]{2,1,0:T(8,128)}), f32[8,256,256]{2,1,0:T(8,128)}) %all-gather.15.cloned.1.call-update) | async-done | bytes 2097168 | tf_op jit(solution)/shard_map/all_gather | solution.py:13
  419.0 1.8 reduce_sum.59
  420.8 2.0 fusion.31
  (49 shorter events, 8.0 us)
Async XLA Ops:
  6.5 33.2 %all-gather.9.cloned.1.call-start = ((), (), s32[]{:S(2)}) async-start(), calls=%async_computation | async-start | bytes 2359296 | tf_op jit(solution)/shard_map/all_gather | solution.py:13
  8.2 175.1 %all-gather.17.cloned.1.call-start = ((), (), s32[]{:S(2)}) async-start(), calls=%async_computation.4 | async-start | bytes 5242880 | tf_op jit(solution)/shard_map/all_gather | solution.py:13
  63.4 39.1 %copy-start.1 = (f32[4,256,256]{2,1,0:T(8,128)S(1)}, f32[4,256,256]{2,1,0:T(8,128)}, u32[]{:S(2)}) copy-start(f32[4,256,256]{2,1,0:T(8,128)} %get-tuple-element.31) | copy-start | bytes 3145732 | tf_op jit(solution)/shard_map/cond
  105.2 107.9 %all-gather.11.cloned.1.call-start = ((), (), s32[]{:S(2)}) async-start(), calls=%async_computation.1 | async-start | bytes 2359296 | tf_op jit(solution)/shard_map/all_gather | solution.py:13
  185.9 28.9 %copy-start = (f32[4,256,256]{2,1,0:T(8,128)S(1)}, f32[4,256,256]{2,1,0:T(8,128)}, u32[]{:S(2)}) copy-start(f32[4,256,256]{2,1,0:T(8,128)} %param.8) | copy-start | bytes 3145732
  186.7 57.9 %all-gather.13.cloned.1.call-start = ((), (), s32[]{:S(2)}) async-start(), calls=%async_computation.2 | async-start | bytes 2359296 | tf_op jit(solution)/shard_map/all_gather | solution.py:13
  216.7 172.6 %all-gather.19.cloned.1.call-start = ((), (), s32[]{:S(2)}) async-start(), calls=%async_computation.5 | async-start | bytes 5242880 | tf_op jit(solution)/shard_map/all_gather | solution.py:13
  246.1 172.9 %all-gather.15.cloned.1.call-start = ((), (), s32[]{:S(2)}) async-start(), calls=%async_computation.3 | async-start | bytes 2359296 | tf_op jit(solution)/shard_map/all_gather | solution.py:13
Sparse Core Ops, SparseCore 0:
  9.2 30.4 all-gather.8
  105.3 77.9 all-gather.16
  186.8 26.2 all-gather.10
  216.8 27.7 all-gather.12
  246.2 142.9 all-gather.18
  392.7 26.2 all-gather.14
